TPU v7x, 32 devices: a whole 2x2x4 slice. The times are simulated.
32 devices in a mesh: seq: 8 (over z, y), tensor: 4 (over x, core).
Axes of the slice: x: 2, y: 2, z: 4, core: 2. Of those that a mesh axis runs over, the one named last changes fastest.
Arguments:
- layer_input: bfloat16 [2048, 4096], P('seq', 'tensor'), may hold values from -6 to 6
- norm_gain: float32 [4096], replicated, may hold values from 0.1 to 1.9
- in_weights: bfloat16 [2, 4096, 2048], P(None, None, 'tensor'), may hold values from -0.09375 to 0.09375
- conv_weight: float32 [4, 2048], P(None, 'tensor'), may hold values from -4 to 4
- conv_bias: float32 [2048], P('tensor'), may hold values from -3 to 3
- gate_weights: bfloat16 [2, 8, 256, 256], P(None, 'tensor'), may hold values from -0.375 to 0.375
- gate_bias: float32 [2, 2048], P(None, 'tensor'), may hold values from -4 to 4
- decay_rate: float32 [2048], P('tensor'), may hold values from 1e-06 to 0.03, as said below
- out_weight: bfloat16 [2048, 4096], P('tensor'), may hold values from -0.1875 to 0.1875
- mlp_gain: float32 [4096], replicated, may hold values from 0.1 to 1.9
- mlp_in: bfloat16 [2, 4096, 6144], P(None, 'seq', 'tensor'), may hold values from -0.09375 to 0.09375
- mlp_out: bfloat16 [6144, 4096], P('tensor', 'seq'), may hold values from -0.109375 to 0.109375
Outputs:
- block_output: bfloat16 [2048, 4096], P('seq', 'tensor')
Inputs may be any that keep to these rules, and one draw needn't show every extreme that they name: `decay_rate`: every rate is positive.
All inputs are finite; a program needn't handle non-finite values.
Results may differ from a plain program's by a relative error of at most 0.015.
Values may be sent and summed in bfloat16 or wider, within the bound.
A program may use at most 128 MiB of HBM per device.

v0:
```python
import jax
import jax.numpy as jnp
from jax import lax
from jax.sharding import PartitionSpec as P


def shifted(value, axis, steps):
    count = lax.axis_size(axis)
    first, last = (max(0, -steps), min(count, count - steps))
    return lax.ppermute(value, axis, [(source, source + steps) for source in range(first, last)])


def prefix(value, axis, combine, identity):
    size, here = (lax.axis_size(axis), lax.axis_index(axis))
    everything = jax.tree.map(lambda part: lax.all_gather(part, axis), value)
    start = jax.tree.map(
        lambda part, zero: jnp.broadcast_to(jnp.asarray(zero, part.dtype), part.shape),
        value,
        identity,
    )

    def hop(k, before):
        reached = k < here
        new = combine(before, jax.tree.map(lambda part: part[k], everything))
        return jax.tree.map(lambda a, b: jnp.where(reached, a, b), new, before)

    return lax.fori_loop(0, size, hop, start)


def rms_scale(rows, gain):
    values = rows.astype(jnp.float32)
    mean_square = jnp.mean(values * values, axis=-1, keepdims=True)
    return (values * lax.rsqrt(mean_square + 1e-06) * gain).astype(jnp.bfloat16)


def chain_step(earlier, later):
    return (earlier[0] * later[0], later[0] * earlier[1] + later[1])


def shards(
    layer_input,
    norm_gain,
    in_weights,
    conv_weight,
    conv_bias,
    gate_weights,
    gate_bias,
    decay_rate,
    out_weight,
    mlp_gain,
    mlp_in,
    mlp_out,
):
    whole_rows = lax.all_gather(layer_input, "tensor", axis=1, tiled=True)
    normed = rms_scale(whole_rows, norm_gain)
    branch_x = jnp.dot(normed, in_weights[0], preferred_element_type=jnp.float32).astype(
        jnp.bfloat16
    )
    branch_y = jax.nn.gelu(
        jnp.dot(normed, in_weights[1], preferred_element_type=jnp.float32), approximate=True
    )
    num_tokens = branch_x.shape[0]
    rim_rows = conv_weight.shape[0] - 1
    earlier_rows = shifted(branch_x[num_tokens - rim_rows :], "seq", 1)
    padded = jnp.concatenate([earlier_rows, branch_x], axis=0).astype(jnp.float32)
    convolved = jnp.zeros(branch_x.shape, jnp.float32) + conv_bias
    for tap_index in range(conv_weight.shape[0]):
        start_row = rim_rows - tap_index
        convolved = convolved + conv_weight[tap_index] * padded[start_row : start_row + num_tokens]
    conv_out = convolved.astype(jnp.bfloat16)
    local_blocks = gate_weights.shape[1]
    block_width = gate_weights.shape[2]
    blocks_in = conv_out.reshape(num_tokens, local_blocks, block_width)
    gate_pre = jnp.einsum(
        "tnc,knce->ktne", blocks_in, gate_weights, preferred_element_type=jnp.float32
    )
    gate_pre = gate_pre.reshape(2, num_tokens, local_blocks * block_width) + gate_bias[:, None, :]
    log_decay = -8.0 * jax.nn.sigmoid(gate_pre[0]) * decay_rate
    decay = jnp.exp(log_decay)
    driven = (
        conv_out.astype(jnp.float32)
        * jax.nn.sigmoid(gate_pre[1])
        * jnp.sqrt(-jnp.expm1(2.0 * log_decay))
    )
    cum_decay, cum_state = lax.associative_scan(chain_step, (decay, driven), axis=0)
    identity = (jnp.ones_like(cum_decay[-1]), jnp.zeros_like(cum_state[-1]))
    entering = prefix((cum_decay[-1], cum_state[-1]), "seq", chain_step, identity)
    carried = entering[1]
    state = cum_decay * carried + cum_state
    mixed = (state * branch_y).astype(jnp.bfloat16)
    partial_sums = jnp.dot(mixed, out_weight, preferred_element_type=jnp.float32)
    full_sums = lax.psum(partial_sums.astype(jnp.bfloat16), "tensor").astype(jnp.float32)
    mid_full = (whole_rows.astype(jnp.float32) + full_sums).astype(jnp.bfloat16)
    own_width = layer_input.shape[1]
    residual = lax.dynamic_slice_in_dim(
        mid_full, lax.axis_index("tensor") * own_width, own_width, 1
    )
    mlp_normed = rms_scale(mid_full, mlp_gain)
    gate_up = jnp.einsum(
        "tr,krf->ktf",
        mlp_normed,
        lax.all_gather(mlp_in, "seq", axis=1, tiled=True),
        preferred_element_type=jnp.float32,
    )
    hidden = (jax.nn.gelu(gate_up[0], approximate=True) * gate_up[1]).astype(jnp.bfloat16)
    down_terms = jnp.dot(
        hidden,
        lax.all_gather(mlp_out, "seq", axis=1, tiled=True),
        preferred_element_type=jnp.float32,
    )
    down_share = lax.psum_scatter(
        down_terms.astype(jnp.bfloat16), "tensor", scatter_dimension=1, tiled=True
    ).astype(jnp.float32)
    return (residual.astype(jnp.float32) + down_share).astype(jnp.bfloat16)


def solution(mesh):
    return jax.shard_map(
        shards,
        mesh=mesh,
        in_specs=(
            P("seq", "tensor"),
            P(),
            P(None, None, "tensor"),
            P(None, "tensor"),
            P("tensor"),
            P(None, "tensor", None, None),
            P(None, "tensor"),
            P("tensor"),
            P("tensor", None),
            P(),
            P(None, "seq", "tensor"),
            P("tensor", "seq"),
        ),
        out_specs=P("seq", "tensor"),
        check_vma=False,
    )
```

profile of v0, /device:TPU:0, one launch (start us, length us, event | category | flops | bytes accessed | tf_op | source)
XLA Modules:
  0.0 835.9 jit_solution(12491428809460878877)
XLA Ops:
  7.4 0.7 all-gather.6.cloned.1.call-update
  8.1 0.9 fusion.115
  9.0 26.0 %all-gather.6.cloned.1.call-done = bf16[256,4096]{1,0:T(8,128)(2,1)} async-done(((bf16[256,1024]{1,0:T(8,128)(2,1)}), bf16[256,4096]{1,0:T(8,128)(2,1)}) %all-gather.6.cloned.1.call-update) | async-done | bytes 2097168 | tf_op jit(solution)/shard_map/all_gather | solution.py:54
  35.0 2.1 fusion.3
  37.2 4.1 fusion.26
  41.3 3.4 collective-permute-start
  44.7 1.3 collective-permute-done
  46.1 0.3 fusion.73
  46.5 0.3 convolution_bitcast_fusion.1
  46.8 0.6 copy.18
  47.4 0.8 reshape.41
  48.3 0.1 broadcast_add_fusion
  48.4 0.8 fusion.91
  49.2 0.3 slice.293
  49.5 0.3 slice.294
  49.8 0.3 slice.332
  50.2 0.3 slice.333
  50.6 0.1 slice.296
  50.7 0.1 slice.297
  50.8 0.1 slice.335
  50.9 0.1 slice.336
  52.0 0.2 slice.326
  52.2 0.2 slice.365
  52.4 1.4 slice.328
  53.8 1.4 slice.367
  56.2 1.7 pad.129
  58.1 2.0 add_multiply_fusion.1
  60.2 1.7 pad.128
  61.8 0.7 add_bitcast_fusion
  62.5 27.9 %all-gather.1 = f32[8,1,512]{2,1,0:T(1,128)S(1)} all-gather(f32[1,1,512]{2,1,0:T(1,128)S(1)} %add_bitcast_fusion), channel_id=1, replica_groups=mesh['seq'=8,'tensor'=4] {'seq'}, dimensions={0}, use_global_device_ids=true | all-gather | bytes 18432 | tf_op jit(solution)/shard_map/all_gather | solution.py:15
  90.4 1.6 pad.113
  92.1 1.0 pad_maximum_fusion
  93.1 1.7 pad.112
  94.7 0.7 add_bitcast_fusion.1
  95.5 26.1 %all-gather = f32[8,1,512]{2,1,0:T(1,128)S(1)} all-gather(f32[1,1,512]{2,1,0:T(1,128)S(1)} %add_bitcast_fusion.1), channel_id=1, replica_groups=mesh['seq'=8,'tensor'=4] {'seq'}, dimensions={0}, use_global_device_ids=true | all-gather | bytes 18432 | tf_op jit(solution)/shard_map/all_gather | solution.py:15
  121.6 0.4 while.14
  122.0 7.9 convolution_convert_fusion.1
  130.0 0.5 all-gather.8.cloned.1.call-update
  130.6 0.5 all-gather.10.cloned.1.call-update
  131.2 0.2 reduce-scatter.2.cloned.1.call-start
  131.4 46.4 %all-reduce.34.cloned.1.call-done = bf16[256,4096]{1,0:T(8,128)(2,1)} async-done(((bf16[256,4096]{1,0:T(8,128)(2,1)}), bf16[256,4096]{1,0:T(8,128)(2,1)}) %all-reduce.34.cloned.1.call-update) | async-done | bytes 2097168 | tf_op jit(solution)/shard_map/psum | solution.py:92
  177.8 3.9 fusion
  181.7 427.0 %all-gather.8.cloned.1.call-done = bf16[2,4096,1536]{2,1,0:T(8,128)(2,1)} async-done(((bf16[2,512,1536]{2,1,0:T(8,128)(2,1)}), bf16[2,4096,1536]{2,1,0:T(8,128)(2,1)}) %all-gather.8.cloned.1.call-update) | async-done | bytes 25165840 | tf_op jit(solution)/shard_map/all_gather | solution.py:102
  608.7 13.4 %convolution_bitcast_fusion = f32[2,256,1536]{2,1,0:T(8,128)} fusion(bf16[2,4096,1536]{2,1,0:T(8,128)(2,1)} %all-gather.8.cloned.1.call-done, bf16[256,4096]{1,0:T(8,128)(2,1)} %get-tuple-element.129, f32[4096]{0:T(1024)S(1)} %copy-done.8, f32[256]{0:T(256)S(1)} %add_rsqrt_fusion), kind=kOutput, calls=%fused_computation.23 | convolution fusion | flops 6446645248 | bytes 30426112 | tf_op jit(solution)/shard_map/tr,krf->ktf/dot_general | solution.py:99
  622.1 164.4 %all-gather.10.cloned.1.call-done = bf16[1536,4096]{1,0:T(8,128)(2,1)} async-done(((bf16[1536,512]{1,0:T(8,128)(2,1)}), bf16[1536,4096]{1,0:T(8,128)(2,1)}) %all-gather.10.cloned.1.call-update) | async-done | bytes 12582928 | tf_op jit(solution)/shard_map/all_gather | solution.py:108
  786.5 10.6 %convolution_convert_fusion = bf16[256,4096]{1,0:T(8,128)(2,1)} fusion(bf16[1536,4096]{1,0:T(8,128)(2,1)} %all-gather.10.cloned.1.call-done, f32[2,256,1536]{2,1,0:T(8,128)} %convolution_bitcast_fusion), kind=kOutput, calls=%fused_computation.8 | convolution fusion | flops 3226206208 | bytes 17825792 | tf_op jit(solution)/shard_map/dot_general | solution.py:106
  797.1 29.5 %reduce-scatter.2.cloned.1.call-done = bf16[256,1024]{1,0:T(8,128)(2,1)} async-done(((bf16[256,4096]{1,0:T(8,128)(2,1)}), bf16[256,1024]{1,0:T(8,128)(2,1)}) %reduce-scatter.2.cloned.1.call-update) | async-done | bytes 524304 | tf_op jit(solution)/shard_map/reduce_scatter | solution.py:111
  826.6 2.2 add_convert_fusion
  (152 shorter events, 2.3 us)
Async XLA Ops:
  7.4 39.1 %copy-start = (bf16[2,2,256,256]{3,2,1,0:T(8,128)(2,1)S(1)}, bf16[2,2,256,256]{3,2,1,0:T(8,128)(2,1)}, u32[]{:S(2)}) copy-start(bf16[2,2,256,256]{3,2,1,0:T(8,128)(2,1)} %param.19) | copy-start | bytes 1572868
  7.4 27.7 %all-gather.6.cloned.1.call-start = ((), (), s32[]{:S(2)}) async-start(), calls=%async_computation.1 | async-start | bytes 2621440 | tf_op jit(solution)/shard_map/all_gather | solution.py:54
  8.1 169.7 %all-reduce.34.cloned.1.call-start = ((), (), s32[]{:S(2)}) async-start(), calls=%async_computation.2 | async-start | bytes 4194304 | tf_op jit(solution)/shard_map/psum | solution.py:92
  37.1 7.6 copy-start.6
  37.1 9.0 %copy-start.4 = (f32[512]{0:T(512)S(1)}, f32[512]{0:T(512)}, u32[]{:S(2)}) copy-start(f32[512]{0:T(512)} %param.18) | copy-start | bytes 6148
  41.3 4.7 collective-permute-start
  46.4 1.8 copy-start.5
  58.1 63.9 %copy-start.2 = (bf16[256,4096]{1,0:T(8,128)(2,1)S(1)}, bf16[256,4096]{1,0:T(8,128)(2,1)}, u32[]{:S(2)}) copy-start(bf16[256,4096]{1,0:T(8,128)(2,1)} %all-gather.6.cloned.1.call-done) | copy-start | bytes 6291460
  58.1 63.9 %copy-start.7 = (f32[4096]{0:T(1024)S(1)}, f32[4096]{0:T(1024)}, u32[]{:S(2)}) copy-start(f32[4096]{0:T(1024)} %param.15) | copy-start | bytes 49156
  60.1 61.9 %copy-start.3 = (f32[256,512]{1,0:T(8,128)S(1)}, f32[256,512]{1,0:T(8,128)}, u32[]{:S(2)}) copy-start(f32[256,512]{1,0:T(8,128)} %pad.129) | copy-start | bytes 1572868
  130.0 478.7 %all-gather.8.cloned.1.call-start = ((), (), s32[]{:S(2)}) async-start(), calls=%async_computation.3 | async-start | bytes 28311552 | tf_op jit(solution)/shard_map/all_gather | solution.py:102
  130.6 656.0 %all-gather.10.cloned.1.call-start = ((), (), s32[]{:S(2)}) async-start(), calls=%async_computation.4 | async-start | bytes 14155776 | tf_op jit(solution)/shard_map/all_gather | solution.py:108
  131.2 477.6 %copy-start.8 = (f32[4096]{0:T(1024)S(1)}, f32[4096]{0:T(1024)}, u32[]{:S(2)}) copy-start(f32[4096]{0:T(1024)} %param.23) | copy-start | bytes 49156
  131.2 695.4 %reduce-scatter.2.cloned.1.call-start = ((), (), s32[]{:S(2)}) async-start(), calls=%async_computation.5 | async-start | bytes 2621440 | tf_op jit(solution)/shard_map/reduce_scatter | solution.py:111
  786.5 42.3 %copy-start.1 = (bf16[2,2,256,256]{3,2,1,0:T(8,128)(2,1)S(1)}, bf16[2,2,256,256]{3,2,1,0:T(8,128)(2,1)}, u32[]{:S(2)}) copy-start(bf16[2,2,256,256]{3,2,1,0:T(8,128)(2,1)} %param.19) | copy-start | bytes 1572868
Sparse Core Ops, SparseCore 0:
  9.7 25.2 all-gather.5
  130.1 47.6 all-reduce.33
  797.2 29.3 reduce-scatter.1
Sparse Core Ops, SparseCore 1:
  132.0 476.6 all-gather.7
  610.6 175.9 all-gather.9
where the time goes:
time: 836 us
  waiting for transfers between devices  696 us (83%)
  blocking collectives  54 us (6%)
  matrix products  36.4 us (4%)
  between operations  15.4 us (2%)
  local copies, waits for them, and re-layouts  15.1 us (2%)
  other arithmetic  14.7 us (2%)
    all_gather x1, waiting for transfers between devices, shards(): lax.all_gather(mlp_in, 'seq', axis=1, tiled=True)  427 us
    all_gather x1, waiting for transfers between devices, shards(): lax.all_gather(mlp_out, 'seq', axis=1, tiled=True)  164 us
    all_gather x2, blocking collectives, prefix(): everything = jax.tree.map(lambda part: lax.all_gather(part, axis), value)  54 us
    psum x1, waiting for transfers between devices, shards(): lax.psum(partial_sums.astype(jnp.bfloat16), 'tensor').astype(jnp.float32)  46.4 us
    reduce_scatter x1, waiting for transfers between devices, shards(): lax.psum_scatter(down_terms.astype(jnp.bfloat16), 'tensor', scatter_dimen...  29.5 us
    all_gather x1, waiting for transfers between devices, shards(): whole_rows = lax.all_gather(layer_input, 'tensor', axis=1, tiled=True)  26 us
  transfers between devices with their start and end apart: 6, of which 6 were waited for; matrix products, arithmetic and copies ran while one was open for 2% of the time, Pallas kernels for 0%

commit v1 on v0

--- a/solution.py
+++ b/solution.py
@@ -2,6 +2,19 @@
 import jax.numpy as jnp
 from jax import lax
 from jax.sharding import PartitionSpec as P
+
+
+def gather_around(value, axis, dim):
+    ways = lax.axis_size(axis)
+    up = [(d, (d + 1) % ways) for d in range(ways)]
+    down = [(d, (d - 1) % ways) for d in range(ways)]
+    earlier, later = ([value], [value])
+    for _ in range(ways // 2):
+        earlier.append(lax.ppermute(earlier[-1], axis, up))
+    for _ in range((ways - 1) // 2):
+        later.append(lax.ppermute(later[-1], axis, down))
+    line = jnp.concatenate([*earlier[::-1], *later[1:]], axis=dim)
+    return jnp.roll(line, (lax.axis_index(axis) - ways // 2) * value.shape[dim], axis=dim)
 
 
 def shifted(value, axis, steps):
@@ -99,7 +112,7 @@
     gate_up = jnp.einsum(
         "tr,krf->ktf",
         mlp_normed,
-        lax.all_gather(mlp_in, "seq", axis=1, tiled=True),
+        gather_around(mlp_in, "seq", 1),
         preferred_element_type=jnp.float32,
     )
     hidden = (jax.nn.gelu(gate_up[0], approximate=True) * gate_up[1]).astype(jnp.bfloat16)

time: 836 us -> 798 us (0.955)
  waiting for transfers between devices: 696 us -> 589 us
  local copies, waits for them, and re-layouts: 15.1 us -> 63.6 us
  starting transfers between devices: 3.72 us -> 23.7 us
    ppermute x0 -> x7, waiting for transfers between devices: none -> 531 us  [the longest x4 396 us: gather_around(): earlier.append(lax.ppermute(earlier[-1], axis, up))]
    all_gather x1 -> x0, waiting for transfers between devices: 427 us -> none  [shards(): lax.all_gather(mlp_in, 'seq', axis=1, tiled=True)]
    all_gather x1, waiting for transfers between devices: 164 us -> 0.01 us  [shards(): lax.all_gather(mlp_out, 'seq', axis=1, tiled=True)]
    unnamed x20 -> x48, local copies, waits for them, and re-layouts: 0.05 us -> 48 us
    psum x1, waiting for transfers between devices: 46.4 us -> 0.01 us  [shards(): lax.psum(partial_sums.astype(jnp.bfloat16), 'tensor').astype(jnp.float32)]
    ppermute x0 -> x7, starting transfers between devices: none -> 20.2 us  [the longest x3 14.7 us: gather_around(): later.append(lax.ppermute(later[-1], axis, down))]
  transfers between devices with their start and end apart: 6 -> 12, of which waited for: 6 -> 9; matrix products, arithmetic and copies ran while one was open for 2% -> 8% of each run, Pallas kernels for 0% -> 0%
where the time goes in v1:
time: 798 us; the launch traced here: 797 us
  waiting for transfers between devices  589 us (74%)
  local copies, waits for them, and re-layouts  63.6 us (8%)
  blocking collectives  54 us (7%)
  matrix products  36.7 us (5%)
  starting transfers between devices  23.7 us (3%)
  between operations  15.5 us (2%)
  other arithmetic  13.8 us (2%)
    ppermute x4, waiting for transfers between devices, gather_around(): earlier.append(lax.ppermute(earlier[-1], axis, up))  396 us
    ppermute x3, waiting for transfers between devices, gather_around(): later.append(lax.ppermute(later[-1], axis, down))  135 us
    all_gather x2, blocking collectives, prefix(): everything = jax.tree.map(lambda part: lax.all_gather(part, axis), value)  54 us
    unnamed x48, local copies, waits for them, and re-layouts  48 us
    reduce_scatter x1, waiting for transfers between devices, shards(): lax.psum_scatter(down_terms.astype(jnp.bfloat16), 'tensor', scatter_dimen...  29.9 us
    all_gather x1, waiting for transfers between devices, shards(): whole_rows = lax.all_gather(layer_input, 'tensor', axis=1, tiled=True)  26 us
  transfers between devices with their start and end apart: 12, of which 9 were waited for; matrix products, arithmetic and copies ran while one was open for 8% of the time, Pallas kernels for 0%

profile of v1, /device:TPU:0, one launch (start us, length us, event | category | flops | bytes accessed | tf_op | source)
XLA Modules:
  0.0 796.8 jit_solution(16321595823166893535)
XLA Ops:
  9.0 26.0 %all-gather.5.cloned.1.call-done = bf16[256,4096]{1,0:T(8,128)(2,1)} async-done(((bf16[256,1024]{1,0:T(8,128)(2,1)}), bf16[256,4096]{1,0:T(8,128)(2,1)}) %all-gather.5.cloned.1.call-update) | async-done | bytes 2097168 | tf_op jit(solution)/shard_map/all_gather | solution.py:67
  35.0 2.1 fusion.5
  37.2 4.1 fusion.31
  41.3 3.4 collective-permute-start
  44.8 1.3 collective-permute-done
  52.4 1.4 slice.328
  53.8 1.4 slice.367
  56.2 1.7 pad.129
  58.0 1.9 add_multiply_fusion.1
  60.7 27.9 %all-gather.1 = f32[8,1,512]{2,1,0:T(1,128)S(1)} all-gather(f32[1,1,512]{2,1,0:T(1,128)S(1)} %add_bitcast_fusion), channel_id=1, replica_groups=mesh['seq'=8,'tensor'=4] {'seq'}, dimensions={0}, use_global_device_ids=true | all-gather | bytes 18432 | tf_op jit(solution)/shard_map/all_gather | solution.py:28
  88.6 1.7 pad.113
  92.1 26.1 %all-gather = f32[8,1,512]{2,1,0:T(1,128)S(1)} all-gather(f32[1,1,512]{2,1,0:T(1,128)S(1)} %add_bitcast_fusion.1), channel_id=1, replica_groups=mesh['seq'=8,'tensor'=4] {'seq'}, dimensions={0}, use_global_device_ids=true | all-gather | bytes 18432 | tf_op jit(solution)/shard_map/all_gather | solution.py:28
  118.7 7.8 convolution_convert_fusion.1
  127.1 3.3 copy.23
  130.5 126.7 %collective-permute-done.1 = bf16[2,512,1536]{1,2,0:T(8,128)(2,1)S(1)} collective-permute-done((bf16[2,512,1536]{1,2,0:T(8,128)(2,1)S(1)}, bf16[2,512,1536]{1,2,0:T(8,128)(2,1)S(1)}, u32[]{:S(2)}, u32[]{:S(2)}) %collective-permute-start.1) | collective-permute-done | bytes 3145760 | tf_op jit(solution)/shard_map/ppermute | solution.py:13
  257.2 4.7 collective-permute-start.5
  261.9 181.8 %collective-permute-done.2 = bf16[2,512,1536]{1,2,0:T(8,128)(2,1)S(1)} collective-permute-done((bf16[2,512,1536]{1,2,0:T(8,128)(2,1)S(1)}, bf16[2,512,1536]{1,2,0:T(8,128)(2,1)S(1)}, u32[]{:S(2)}, u32[]{:S(2)}) %collective-permute-start.2) | collective-permute-done | bytes 3145760 | tf_op jit(solution)/shard_map/ppermute | solution.py:13
  443.7 2.9 collective-permute-start.3
  446.6 16.6 %collective-permute-done.5 = bf16[2,512,1536]{1,2,0:T(8,128)(2,1)S(1)} collective-permute-done((bf16[2,512,1536]{1,2,0:T(8,128)(2,1)S(1)}, bf16[2,512,1536]{1,2,0:T(8,128)(2,1)S(1)}, u32[]{:S(2)}, u32[]{:S(2)}) %collective-permute-start.5) | collective-permute-done | bytes 3145760 | tf_op jit(solution)/shard_map/ppermute | solution.py:15
  463.2 7.0 collective-permute-start.6
  470.2 87.3 %collective-permute-done.3 = bf16[2,512,1536]{1,2,0:T(8,128)(2,1)} collective-permute-done((bf16[2,512,1536]{1,2,0:T(8,128)(2,1)S(1)}, bf16[2,512,1536]{1,2,0:T(8,128)(2,1)}, u32[]{:S(2)}, u32[]{:S(2)}) %collective-permute-start.3) | collective-permute-done | bytes 3145760 | tf_op jit(solution)/shard_map/ppermute | solution.py:13
  557.5 2.6 collective-permute-start.4
  560.1 84.0 %collective-permute-done.6 = bf16[2,512,1536]{1,2,0:T(8,128)(2,1)} collective-permute-done((bf16[2,512,1536]{1,2,0:T(8,128)(2,1)S(1)}, bf16[2,512,1536]{1,2,0:T(8,128)(2,1)}, u32[]{:S(2)}, u32[]{:S(2)}) %collective-permute-start.6) | collective-permute-done | bytes 3145760 | tf_op jit(solution)/shard_map/ppermute | solution.py:15
  644.1 3.0 collective-permute-start.7
  647.1 3.2 fusion.2
  650.3 4.5 constant_dynamic-update-slice_fusion.15
  654.9 3.9 constant_dynamic-update-slice_fusion.14
  658.8 1.8 constant_dynamic-update-slice_fusion.13
  660.6 1.2 copy-done.3
  661.8 1.9 constant_dynamic-update-slice_fusion.12
  663.7 1.9 constant_dynamic-update-slice_fusion.11
  665.6 1.1 copy-done.5
  666.7 1.9 constant_dynamic-update-slice_fusion.10
  668.6 3.8 constant_dynamic-update-slice_fusion.9
  672.5 34.5 %collective-permute-done.7 = bf16[2,512,1536]{1,2,0:T(8,128)(2,1)} collective-permute-done((bf16[2,512,1536]{1,2,0:T(8,128)(2,1)}, bf16[2,512,1536]{1,2,0:T(8,128)(2,1)}, u32[]{:S(2)}, u32[]{:S(2)}) %collective-permute-start.7) | collective-permute-done | bytes 3145760 | tf_op jit(solution)/shard_map/ppermute | solution.py:15
  707.0 3.8 constant_dynamic-update-slice_fusion.8
  710.8 3.7 constant_dynamic-update-slice_fusion.7
  714.5 3.8 constant_dynamic-update-slice_fusion.6
  718.3 1.9 constant_dynamic-update-slice_fusion.5
  720.1 1.9 constant_dynamic-update-slice_fusion.4
  722.0 1.8 constant_dynamic-update-slice_fusion.3
  723.9 1.9 constant_dynamic-update-slice_fusion.2
  725.7 3.7 constant_dynamic-update-slice_fusion.1
  729.4 3.8 constant_dynamic-update-slice_fusion
  733.2 13.5 %fusion.15 = f32[2,256,1536]{1,2,0:T(8,128)} fusion(bf16[2,8192,1536]{1,2,0:T(8,128)(2,1)} %constant_dynamic-update-slice_fusion, s32[]{:T(128)S(6)} %select_n.40, bf16[256,4096]{1,0:T(8,128)(2,1)S(1)} %get-tuple-element.129, f32[4096]{0:T(1024)S(1)} %copy-done.14, f32[256]{0:T(256)S(1)} %add_rsqrt_fusion), kind=kOutput, calls=%fused_computation.25 | convolution fusion | flops 6446645248 | bytes 30426116 | tf_op jit(solution)/shard_map/tr,krf->ktf/dot_general | solution.py:112
  746.7 10.9 %convolution_convert_fusion = bf16[256,4096]{1,0:T(8,128)(2,1)} fusion(bf16[1536,4096]{1,0:T(8,128)(2,1)} %all-gather.7.cloned.1.call-done, f32[2,256,1536]{1,2,0:T(8,128)} %fusion.15), kind=kOutput, calls=%fused_computation.10 | convolution fusion | flops 3226206208 | bytes 17825792 | tf_op jit(solution)/shard_map/dot_general | solution.py:119
  757.6 29.9 %reduce-scatter.2.cloned.1.call-done = bf16[256,1024]{1,0:T(8,128)(2,1)} async-done(((bf16[256,4096]{1,0:T(8,128)(2,1)}), bf16[256,1024]{1,0:T(8,128)(2,1)}) %reduce-scatter.2.cloned.1.call-update) | async-done | bytes 524304 | tf_op jit(solution)/shard_map/reduce_scatter | solution.py:124
  787.5 2.2 add_convert_fusion
  (192 shorter events, 12.5 us)
Async XLA Ops:
  7.4 39.1 %copy-start = (bf16[2,2,256,256]{3,2,1,0:T(8,128)(2,1)S(1)}, bf16[2,2,256,256]{3,2,1,0:T(8,128)(2,1)}, u32[]{:S(2)}) copy-start(bf16[2,2,256,256]{3,2,1,0:T(8,128)(2,1)} %param.19) | copy-start | bytes 1572868
  7.4 27.7 %all-gather.5.cloned.1.call-start = ((), (), s32[]{:S(2)}) async-start(), calls=%async_computation.1 | async-start | bytes 2621440 | tf_op jit(solution)/shard_map/all_gather | solution.py:67
  8.1 639.0 %all-reduce.34.cloned.1.call-start = ((), (), s32[]{:S(2)}) async-start(), calls=%async_computation.2 | async-start | bytes 4194304 | tf_op jit(solution)/shard_map/psum | solution.py:105
  37.1 7.6 copy-start.12
  37.1 9.0 %copy-start.10 = (f32[512]{0:T(512)S(1)}, f32[512]{0:T(512)}, u32[]{:S(2)}) copy-start(f32[512]{0:T(512)} %param.18) | copy-start | bytes 6148
  41.3 4.7 collective-permute-start
  46.1 2.1 copy-start.11
  56.2 62.4 %copy-start.8 = (bf16[256,4096]{1,0:T(8,128)(2,1)S(1)}, bf16[256,4096]{1,0:T(8,128)(2,1)}, u32[]{:S(2)}) copy-start(bf16[256,4096]{1,0:T(8,128)(2,1)} %all-gather.5.cloned.1.call-done) | copy-start | bytes 6291460
  56.2 62.4 %copy-start.13 = (f32[4096]{0:T(1024)S(1)}, f32[4096]{0:T(1024)}, u32[]{:S(2)}) copy-start(f32[4096]{0:T(1024)} %param.15) | copy-start | bytes 49156
  126.5 620.2 %all-gather.7.cloned.1.call-start = ((), (), s32[]{:S(2)}) async-start(), calls=%async_computation.3 | async-start | bytes 14155776 | tf_op jit(solution)/shard_map/all_gather | solution.py:121
  127.1 660.4 %reduce-scatter.2.cloned.1.call-start = ((), (), s32[]{:S(2)}) async-start(), calls=%async_computation.4 | async-start | bytes 2621440 | tf_op jit(solution)/shard_map/reduce_scatter | solution.py:124
  130.5 126.7 %collective-permute-start.1 = (bf16[2,512,1536]{1,2,0:T(8,128)(2,1)S(1)}, bf16[2,512,1536]{1,2,0:T(8,128)(2,1)S(1)}, u32[]{:S(2)}, u32[]{:S(2)}) collective-permute-start(bf16[2,512,1536]{1,2,0:T(8,128)(2,1)S(1)} %copy.23), channel_id=1, source_target_pairs={{0,4},{4,8},{8,12},{12,16},{16,20},{20,24},{24,28},{28,0},{1,5},{5... | collective-permute-start | bytes 9437192 | tf_op jit(solution)/shard_map/ppermute | solution.py:13
  257.2 206.0 %copy-start.2 = (bf16[2,512,1536]{1,2,0:T(8,128)(2,1)}, bf16[2,512,1536]{1,2,0:T(8,128)(2,1)S(1)}, u32[]{:S(2)}) copy-start(bf16[2,512,1536]{1,2,0:T(8,128)(2,1)S(1)} %collective-permute-done.1) | copy-start | bytes 9437188
  257.2 186.5 %collective-permute-start.2 = (bf16[2,512,1536]{1,2,0:T(8,128)(2,1)S(1)}, bf16[2,512,1536]{1,2,0:T(8,128)(2,1)S(1)}, u32[]{:S(2)}, u32[]{:S(2)}) collective-permute-start(bf16[2,512,1536]{1,2,0:T(8,128)(2,1)S(1)} %collective-permute-done.1), channel_id=1, source_target_pairs={{0,4},{4,8},{8,12},{12,16},{16,20},{20,24},{24,28},{28,0},{1,5},{5... | collective-permute-start | bytes 9437192 | tf_op jit(solution)/shard_map/ppermute | solution.py:13
  257.2 206.0 %collective-permute-start.5 = (bf16[2,512,1536]{1,2,0:T(8,128)(2,1)S(1)}, bf16[2,512,1536]{1,2,0:T(8,128)(2,1)S(1)}, u32[]{:S(2)}, u32[]{:S(2)}) collective-permute-start(bf16[2,512,1536]{1,2,0:T(8,128)(2,1)S(1)} %copy.23), channel_id=1, source_target_pairs={{0,28},{4,0},{8,4},{12,8},{16,12},{20,16},{24,20},{28,24},{1,29},{... | collective-permute-start | bytes 9437192 | tf_op jit(solution)/shard_map/ppermute | solution.py:15
  443.7 200.4 %copy-start.6 = (bf16[2,512,1536]{1,2,0:T(8,128)(2,1)}, bf16[2,512,1536]{1,2,0:T(8,128)(2,1)S(1)}, u32[]{:S(2)}) copy-start(bf16[2,512,1536]{1,2,0:T(8,128)(2,1)S(1)} %collective-permute-done.2) | copy-start | bytes 9437188
  443.7 113.8 %collective-permute-start.3 = (bf16[2,512,1536]{1,2,0:T(8,128)(2,1)S(1)}, bf16[2,512,1536]{1,2,0:T(8,128)(2,1)}, u32[]{:S(2)}, u32[]{:S(2)}) collective-permute-start(bf16[2,512,1536]{1,2,0:T(8,128)(2,1)S(1)} %collective-permute-done.2), channel_id=1, source_target_pairs={{0,4},{4,8},{8,12},{12,16},{16,20},{20,24},{24,28},{28,0},{1,5},{5... | collective-permute-start | bytes 9437192 | tf_op jit(solution)/shard_map/ppermute | solution.py:13
  463.2 7.0 copy-start.4
  463.2 180.9 %collective-permute-start.6 = (bf16[2,512,1536]{1,2,0:T(8,128)(2,1)S(1)}, bf16[2,512,1536]{1,2,0:T(8,128)(2,1)}, u32[]{:S(2)}, u32[]{:S(2)}) collective-permute-start(bf16[2,512,1536]{1,2,0:T(8,128)(2,1)S(1)} %collective-permute-done.5), channel_id=1, source_target_pairs={{0,28},{4,0},{8,4},{12,8},{16,12},{20,16},{24,20},{28,24},{1,29},{... | collective-permute-start | bytes 9437192 | tf_op jit(solution)/shard_map/ppermute | solution.py:15
  557.5 92.8 %collective-permute-start.4 = (bf16[2,512,1536]{1,2,0:T(8,128)(2,1)}, bf16[2,512,1536]{1,2,0:T(8,128)(2,1)}, u32[]{:S(2)}, u32[]{:S(2)}) collective-permute-start(bf16[2,512,1536]{1,2,0:T(8,128)(2,1)} %collective-permute-done.3), channel_id=1, source_target_pairs={{0,4},{4,8},{8,12},{12,16},{16,20},{20,24},{24,28},{28,0},{1,5},{5... | collective-permute-start | bytes 9437192 | tf_op jit(solution)/shard_map/ppermute | solution.py:13
  644.1 62.8 %collective-permute-start.7 = (bf16[2,512,1536]{1,2,0:T(8,128)(2,1)}, bf16[2,512,1536]{1,2,0:T(8,128)(2,1)}, u32[]{:S(2)}, u32[]{:S(2)}) collective-permute-start(bf16[2,512,1536]{1,2,0:T(8,128)(2,1)} %collective-permute-done.6), channel_id=1, source_target_pairs={{0,28},{4,0},{8,4},{12,8},{16,12},{20,16},{24,20},{28,24},{1,29},{... | collective-permute-start | bytes 9437192 | tf_op jit(solution)/shard_map/ppermute | solution.py:15
  650.3 82.9 %copy-start.9 = (bf16[256,4096]{1,0:T(8,128)(2,1)}, bf16[256,4096]{1,0:T(8,128)(2,1)S(1)}, u32[]{:S(2)}) copy-start(bf16[256,4096]{1,0:T(8,128)(2,1)S(1)} %get-tuple-element.129) | copy-start | bytes 6291460
  654.9 3.9 copy-start.7
  658.8 3.0 copy-start.3
  663.7 3.0 copy-start.5
  729.4 3.8 copy-start.14
  746.7 43.0 %copy-start.1 = (bf16[2,2,256,256]{3,2,1,0:T(8,128)(2,1)S(1)}, bf16[2,2,256,256]{3,2,1,0:T(8,128)(2,1)}, u32[]{:S(2)}) copy-start(bf16[2,2,256,256]{3,2,1,0:T(8,128)(2,1)} %param.19) | copy-start | bytes 1572868
Sparse Core Ops, SparseCore 0:
  9.7 25.2 all-gather.4
  126.6 47.7 all-reduce.33
  757.7 29.7 reduce-scatter.1
Sparse Core Ops, SparseCore 1:
  129.0 388.7 all-gather.6
